TPU v7x, 128 devices: a whole 4x4x4 slice. The times are simulated.
128 devices in a mesh: dev: 128 (over z, y, x, core).
Axes of the slice: x: 4, y: 4, z: 4, core: 2. Of those that a mesh axis runs over, the one named last changes fastest.
Arguments:
- orbitals: bfloat16 [128, 768, 6144], P('dev'), may hold values from -0.21875 to 0.21875
- density_blocks: bfloat16 [512, 16, 128, 128], P('dev'), may hold values from -1.625 to 2.625
- kinetic_blocks: float32 [512, 16, 128, 128], P('dev'), may hold values from -0.6 to 0.6
- hartree: float32 [768, 8, 128], P('dev'), may hold values from -6 to 6
- vectors: bfloat16 [65536, 256], P('dev'), may hold values from -6 to 6
- brick_blocks: int32 [128, 6], replicated, may hold values from 0 to 511, as said below
- neighbours: int32 [512, 16], replicated, may hold values from 0 to 511, as said below
Outputs:
- potential: float32 [768, 8, 128], P('dev')
- hamiltonian: float32 [512, 16, 128, 128], P('dev')
- first_term: bfloat16 [65536, 256], P('dev')
- second_term: bfloat16 [65536, 256], P('dev')
Inputs may be any that keep to these rules, and one draw needn't show every extreme that they name: `brick_blocks`: block b is held by device b // 4. Each brick names 6 different blocks, each held by a device at most 2 indices away from the brick's device, counting cyclically; any two blocks of one brick appear in each other's neighbour lists. `neighbours`: each row names 16 different blocks, the row's own block among them, each held by a device at most 3 indices away from the row's device, counting cyclically.
All inputs are finite; a program needn't handle non-finite values.
Results may differ from a plain program's by a relative error of at most 0.0064.
Values may be sent and summed in bfloat16 or wider, within the bound.
A program may use at most 128 MiB of HBM per device.

v0:
```python
import functools
import math

import jax
import jax.numpy as jnp
from jax import lax
from jax.experimental import pallas as pl
from jax.experimental.pallas import tpu as pltpu
from jax.sharding import PartitionSpec as P

MESH = pl.DeviceIdType.MESH
VMEM = pltpu.VMEM
SMEM = pltpu.SMEM
F32 = jnp.float32
BF16 = jnp.bfloat16

density_floor = 0.1
grid_step = 0.04
volume_step = 0.25
kappa_pbe = 0.804
mu_pbe = 0.2195

BLOCK = 128
OWN = 4
WIDTH = 6
NEIGH = 16
PLANES = 6
LINES = 8
ROW = 128
PLANE = LINES * ROW
VEC = 256
STEP = 2
SECOND_LIMIT = 8_000_000
PREP_LIMIT = 60_900_000

FLOWS = 5
SLOTS = FLOWS * OWN
BACK = (0, 1, 3, 2)

T_ROW = 0
T_VALID = T_ROW + SLOTS + 1
T_PLACE = T_VALID + SLOTS + 1
T_SLOT = T_PLACE + (SLOTS + 1) * WIDTH
T_PERM = T_SLOT + WIDTH
T_POS = T_PERM + WIDTH
T_ITEM = T_POS + WIDTH
T_LOOK = T_ITEM + SLOTS
T_SIZE = T_LOOK + OWN * NEIGH
SPAN = 9 * OWN


def around(me, count):
    core = lax.rem(me, 2)
    step = 1 - 2 * core
    partner = me + step
    near = lax.rem(me - step + count, count)
    ahead = lax.rem(me + 2 * step + count, count)
    behind = lax.rem(me - 2 * step + count, count)
    return step, partner, near, ahead, behind


def greet(devices):
    barrier = pltpu.get_barrier_semaphore()
    for device in devices:
        pl.semaphore_signal(barrier, inc=1, device_id=(device,), device_id_type=MESH)


def await_greetings(number):
    pl.semaphore_wait(pltpu.get_barrier_semaphore(), number)


def remote(src, dst, send_sem, recv_sem, device):
    return pltpu.make_async_remote_copy(
        src_ref=src,
        dst_ref=dst,
        send_sem=send_sem,
        recv_sem=recv_sem,
        device_id=(device,),
        device_id_type=MESH,
    )


def row_copies(send, place, send_sems, recv_sems, caps, devices):
    sends, receives = {}, {}
    for flow in range(4):
        back = BACK[flow]
        if caps[flow]:
            slots = pl.ds(flow * OWN, caps[flow])
            there = place(back, caps[flow])
            sends[flow] = remote(
                send.at[slots], there, send_sems.at[flow], recv_sems.at[back], devices[flow]
            )
        if caps[back]:
            slots = pl.ds(flow * OWN, caps[back])
            here = place(flow, caps[back])
            receives[flow] = remote(
                send.at[slots], here, send_sems.at[flow], recv_sems.at[flow], devices[flow]
            )
    return sends, receives


def vector_copies(held, send_sems, recv_sems, me, count, far):
    step, partner, near, ahead, behind = around(me, count)
    up = lax.rem(me + 2, count)
    down = lax.rem(me + count - 2, count)

    def piece(delta):
        return held.at[pl.ds((delta + 3) * OWN, OWN)]

    def copy(src_delta, dst_delta, sem, device):
        return remote(
            piece(src_delta), piece(dst_delta), send_sems.at[sem], recv_sems.at[sem], device
        )

    first = [copy(0, -2, 0, up), copy(0, 2, 1, down), copy(0, -step, 2, partner)]
    second = [copy(-2, -2 - step, 3, partner), copy(2, 2 - step, 4, partner)]
    third = []
    if far:
        third.append(copy(2 * step, 3 * step, 5, near))
    return first, second, third


def central_roll(field, axis, size):
    after = pltpu.roll(field, size - 1, axis)
    before = pltpu.roll(field, 1, axis)
    return (after - before) / (2.0 * grid_step)


def energy_terms(values, squares):
    slater = 0.75 * (3.0 / math.pi) ** (1.0 / 3.0)
    scale = 4.0 * (3.0 * math.pi**2) ** (2.0 / 3.0)
    cube = jnp.exp(jnp.log(values) * (1.0 / 3.0))
    four = cube * values
    reduced = squares / (scale * four * four)
    inner = 1.0 + mu_pbe * reduced / kappa_pbe
    factor = 1.0 + kappa_pbe - kappa_pbe / inner
    slope = mu_pbe / (inner * inner)
    e_dens = -slater * cube * ((4.0 / 3.0) * factor - (8.0 / 3.0) * reduced * slope)
    e_sigma = -slater * slope / (scale * four)
    return e_dens, e_sigma


def prep_kernel(
    count, bricks, neigh, brick_rows, neigh_rows, blocks_hbm, hartree_hbm, vec_hbm,
    table, level_ref, blocks, hartree, vec, inverse, sems,
):
    loads = [
        pltpu.make_async_copy(src, dst, sems.at[i])
        for i, (src, dst) in enumerate(
            ((blocks_hbm, blocks), (hartree_hbm, hartree), (vec_hbm, vec))
        )
    ]
    for load in loads:
        load.start()
    me = lax.axis_index("dev")
    _, *others = around(me, count)
    devices = others + [me]
    blocks = count * OWN

    width = brick_rows.shape
    lists = brick_rows[...]
    brick = lax.broadcasted_iota(jnp.int32, width, 1)
    owner = lists // OWN
    rank = jnp.ones(width, jnp.int32)
    for j in range(WIDTH):
        one = jnp.broadcast_to(lists[j : j + 1], width)
        rank += jnp.where((one // OWN == owner) & (one < lists), 1, 0)
    delta = owner - brick
    delta = jnp.where(delta > count // 2, delta - count, delta)
    delta = jnp.where(delta < -(count // 2), delta + count, delta)
    sided = jnp.where(brick % 2 == 0, delta, -delta)
    near_rows = jnp.max(jnp.where(sided < 0, rank, 0))
    far_rows = jnp.max(jnp.where(sided > 1, rank, 0))
    used = neigh_rows[...] // (2 * OWN)
    home = lax.broadcasted_iota(jnp.int32, used.shape, 1) // (2 * OWN)
    apart = jnp.abs(used - home)
    apart = jnp.minimum(apart, count // 2 - apart)
    chips = jnp.max(apart)
    fits = (near_rows <= 1) & (far_rows == 0) & (chips <= 1)
    level_ref[0] = jnp.where(fits, 0, 1).astype(jnp.int32)

    def near_id(block):
        gap = block - (me - 4) * OWN
        gap = jnp.where(gap < 0, gap + blocks, gap)
        return jnp.where(gap >= blocks, gap - blocks, gap)

    for q in range(T_SIZE):
        table[q] = 0
    for s in range(OWN):
        for k in range(NEIGH):
            gap = near_id(neigh[k, me * OWN + s])
            inverse[s * SPAN + gap] = k
            table[T_LOOK + s * NEIGH + k] = gap - OWN
    for f in range(FLOWS):
        listed = [bricks[p, devices[f]] for p in range(WIDTH)]
        gaps = [near_id(b) for b in listed]
        found = 0
        for s in range(OWN):
            hit = listed[0] == me * OWN + s
            for p in range(1, WIDTH):
                hit = hit | (listed[p] == me * OWN + s)
            slot = jnp.where(hit, f * OWN + found, SLOTS)
            table[T_ROW + slot] = s
            table[T_VALID + slot] = 1
            for p in range(WIDTH):
                gap = jnp.where(hit, s * SPAN + gaps[p], 0)
                table[T_PLACE + slot * WIDTH + p] = inverse[gap]
            found = found + jnp.where(hit, 1, 0)

    listed = [bricks[p, me] for p in range(WIDTH)]
    owners = [b // OWN for b in listed]
    local = [jnp.where(o // 2 == me // 2, 1, 0) for o in owners]
    ahead = 0
    behind = sum(local)
    for j in range(WIDTH):
        slot = 0
        for f in range(FLOWS):
            slot = jnp.where(owners[j] == devices[f], f * OWN, slot)
        for i in range(WIDTH):
            if i != j:
                slot = slot + jnp.where((owners[i] == owners[j]) & (listed[i] < listed[j]), 1, 0)
        place = jnp.where(local[j] == 1, ahead, behind)
        ahead = ahead + local[j]
        behind = behind + 1 - local[j]
        table[T_SLOT + place] = slot
        table[T_PERM + place] = j
        table[T_POS + j] = place
        table[T_ITEM + slot] = place
    for load in loads:
        load.wait()


def prep_stage(count, brick_blocks, neighbours, density_blocks, hartree, vectors):
    brick_blocks, neighbours = brick_blocks.T, neighbours.T
    smem_spec = pl.BlockSpec(memory_space=SMEM)
    vmem_spec = pl.BlockSpec(memory_space=VMEM)
    hbm_spec = pl.BlockSpec(memory_space=pltpu.HBM)
    return pl.pallas_call(
        functools.partial(prep_kernel, count),
        out_shape=(
            jax.ShapeDtypeStruct((T_SIZE,), jnp.int32),
            jax.ShapeDtypeStruct((1,), jnp.int32),
            jax.ShapeDtypeStruct(density_blocks.shape, BF16),
            jax.ShapeDtypeStruct(hartree.shape, F32),
            jax.ShapeDtypeStruct(vectors.shape, BF16),
        ),
        in_specs=[smem_spec, smem_spec, vmem_spec, vmem_spec] + [hbm_spec] * 3,
        out_specs=(smem_spec, smem_spec) + (vmem_spec,) * 3,
        scratch_shapes=[SMEM((OWN * SPAN,), jnp.int32), pltpu.SemaphoreType.DMA((3,))],
        compiler_params=pltpu.CompilerParams(vmem_limit_bytes=PREP_LIMIT),
        name="prep",
    )(brick_blocks, neighbours, brick_blocks, neighbours, density_blocks, hartree, vectors)


def brick_kernel(
    caps,
    far,
    split,
    count,
    table,
    orb_hbm,
    blocks,
    kinetic_hbm,
    hartree_ref,
    vec_ref,
    pot_ref,
    terms,
    held,
    kinetic,
    coarse,
    orb,
    send,
    close,
    cross,
    mat,
    inner,
    dens,
    outer_part,
    inner_part,
    part16,
    tsend,
    local_sems,
    send_sems,
    recv_sems,
    halo_send_sems,
    halo_recv_sems,
    term_send_sems,
    term_recv_sems,
    vec_send_sems,
    vec_recv_sems,
):
    me = lax.axis_index("dev")
    step, partner, near, ahead, behind = around(me, count)
    devices = (partner, near, ahead, behind)
    greet(devices)
    orb_load = pltpu.make_async_copy(orb_hbm, orb, local_sems.at[1])
    orb_load.start()
    own_vec = pltpu.make_async_copy(vec_ref, held.at[pl.ds(3 * OWN, OWN)], local_sems.at[2])
    own_vec.start()

    def fill(target, base, flow, slots):
        def body(i, carry):
            slot = flow * OWN + i
            row = table[T_ROW + slot]
            for p in range(WIDTH):
                target[base + i, p] = blocks[row, table[T_PLACE + slot * WIDTH + p]]
            return carry

        lax.fori_loop(0, slots, body, 0)

    def row_place(flow, slots):
        if flow == 0:
            return close.at[pl.ds(0, slots)]
        return cross.at[pl.ds((flow - 1) * OWN, slots)]

    sends, receives = row_copies(send, row_place, send_sems, recv_sems, caps, devices)
    for flow in (1, 2, 3):
        fill(send, flow * OWN, flow, caps[flow])
    await_greetings(4)
    for flow in (1, 2, 3):
        if flow in sends:
            sends[flow].start()
    fill(send, 0, 0, OWN)
    sends[0].start()
    fill(close, OWN, 4, OWN)
    kinetic_load = pltpu.make_async_copy(kinetic_hbm, kinetic, local_sems.at[3])
    kinetic_load.start()

    def assemble(rows, all_here):
        for a in rows:
            slot = table[T_SLOT + a]
            far_slot = jnp.clip(slot - OWN, 0, 3 * OWN - 1)
            is_far = (slot >= OWN) & (slot < 4 * OWN)
            close_slot = jnp.where(slot < OWN, slot, jnp.maximum(slot - 3 * OWN, 0))
            for p in range(WIDTH):
                tile = close[close_slot, p]
                if all_here:
                    tile = jnp.where(is_far, cross[far_slot, p], tile)
                mat[pl.ds(a * BLOCK, BLOCK), pl.ds(p * BLOCK, BLOCK)] = tile

    def await_cross():
        for flow in (1, 2, 3):
            if flow in receives:
                receives[flow].wait_recv()

    own_vec.wait()
    first, second, third = vector_copies(held, vec_send_sems, vec_recv_sems, me, count, far)

    def row_terms(x, begin, end):
        cols = pl.ds(pl.multiple_of(x * PLANE, PLANE), PLANE)
        here = orb[:, :, cols].reshape(WIDTH * BLOCK, PLANE)
        rows = pl.ds(begin * BLOCK, (end - begin) * BLOCK)
        mixed = jnp.dot(mat[rows, :], here, preferred_element_type=F32)
        total = None
        for a in range(begin, end):
            mine = orb[table[T_PERM + a], :, cols].astype(F32)
            term = mixed[(a - begin) * BLOCK : (a - begin + 1) * BLOCK] * mine
            total = term if total is None else total + term
        return jnp.sum(total, axis=0, keepdims=True)

    def store_line(x, line):
        for y in range(LINES):
            dens[x + 2, pl.ds(y, 1), :] = jnp.maximum(
                line[:, y * ROW : (y + 1) * ROW], density_floor
            )

    def plane_of(q):
        return jnp.where(q >= 4, q - 2, q + 2 * (q // 2))

    def inner_body(q, carry):
        inner[q] = row_terms(plane_of(q), 0, 4)
        return carry

    def outer_body(q, carry):
        x = plane_of(q)
        store_line(x, inner[q] + row_terms(x, 4, WIDTH))
        return carry

    receives[0].wait_recv()
    if not split:
        await_cross()
    assemble(range(4), not split)
    orb_load.wait()
    lax.fori_loop(0, 5, inner_body, 0)
    if split:
        await_cross()
    assemble(range(4, WIDTH), True)
    lax.fori_loop(0, 4, outer_body, 0)
    below = lax.rem(me + count - 1, count)
    above = lax.rem(me + 1, count)
    halo_down = remote(
        dens.at[pl.ds(2, 2)], dens.at[pl.ds(8, 2)], halo_send_sems.at[0], halo_recv_sems.at[0], below
    )
    halo_up = remote(
        dens.at[pl.ds(6, 2)], dens.at[pl.ds(0, 2)], halo_send_sems.at[1], halo_recv_sems.at[1], above
    )
    halo_down.start()
    halo_up.start()
    for copy in first:
        copy.start()
    lax.fori_loop(5, 6, inner_body, 0)
    lax.fori_loop(4, 6, outer_body, 0)
    outer_part[...] = jnp.zeros_like(outer_part)
    inner_part[...] = jnp.zeros_like(inner_part)
    halo_down.wait()
    halo_up.wait()

    field = dens[...]
    mid = field[1:9]
    grad_x = (field[2:10] - field[0:8]) / (2.0 * grid_step)
    grad_y = central_roll(mid, 1, LINES)
    grad_z = central_roll(mid, 2, ROW)
    e_dens, e_sigma = energy_terms(mid, grad_x * grad_x + grad_y * grad_y + grad_z * grad_z)
    twice = 2.0 * e_sigma
    flux_x = twice * grad_x
    divergence = (flux_x[2:8] - flux_x[0:6]) / (2.0 * grid_step)
    divergence = divergence + central_roll((twice * grad_y)[1:7], 1, LINES)
    divergence = divergence + central_roll((twice * grad_z)[1:7], 2, ROW)
    pot_ref[...] = hartree_ref[...] + e_dens[1:7] - divergence

    span = STEP * PLANE

    def scale_of(q):
        lines = [
            pot_ref[q * STEP + x, pl.ds(y, 1), :] for x in range(STEP) for y in range(LINES)
        ]
        return jnp.concatenate(lines, axis=1)

    def rows_of(a, cols):
        pair = [orb[table[T_PERM + a], :, cols], orb[table[T_PERM + a + 1], :, cols]]
        return jnp.concatenate(pair, axis=0)

    def product(left, right):
        return lax.dot_general(
            left, right, (((1,), (1,)), ((), ())), preferred_element_type=F32
        )

    def outer_terms(q, carry):
        cols = pl.ds(pl.multiple_of(q * span, span), span)
        weighted = (rows_of(4, cols).astype(F32) * scale_of(q)).astype(BF16)
        every = orb[:, :, cols].reshape(WIDTH * BLOCK, span)
        outer_part[...] += product(every, weighted).reshape(outer_part.shape)
        return carry

    def inner_terms(q, carry):
        cols = pl.ds(pl.multiple_of(q * span, span), span)
        scale = scale_of(q)
        top, low = rows_of(0, cols), rows_of(2, cols)
        inner_part[pl.ds(0, 256), pl.ds(0, 256)] += product(
            top, (top.astype(F32) * scale).astype(BF16)
        )
        weighted = (low.astype(F32) * scale).astype(BF16)
        both = jnp.concatenate([top, low], axis=0)
        inner_part[:, pl.ds(256, 256)] += product(both, weighted)
        return carry

    def rounded(tile):
        return (volume_step * tile).astype(BF16)

    lax.fori_loop(0, PLANES // STEP, outer_terms, 0)
    for a in (4, 5):
        side = pl.ds((a - 4) * BLOCK, BLOCK)
        for b in range(WIDTH):
            tile = outer_part[table[T_PERM + b], :, side]
            part16[a, b] = rounded(tile.T)
            if b < 4:
                part16[b, a] = rounded(tile)

    def pick(flow, slots):
        def body(i, carry):
            slot = flow * OWN + i
            row = table[T_ITEM + slot]
            for p in range(WIDTH):
                tsend[slot, p] = part16[row, table[T_POS + p]]
            return carry

        lax.fori_loop(0, slots, body, 0)

    def term_place(flow, slots):
        return terms.at[pl.ds(flow * OWN, slots)]

    term_caps = [caps[BACK[flow]] for flow in range(4)]
    term_sends, term_receives = row_copies(
        tsend, term_place, term_send_sems, term_recv_sems, term_caps, devices
    )

    def send_cross():
        for flow in (1, 3, 2):
            if flow in term_sends:
                pick(flow, term_caps[flow])
                term_sends[flow].start()

    if split:
        send_cross()
    for copy in first:
        copy.wait()
    for copy in second + third:
        copy.start()
    lax.fori_loop(0, PLANES // STEP, inner_terms, 0)
    for a in range(4):
        for b in range(4):
            if a // 2 <= b // 2:
                tile = inner_part[pl.ds(a * BLOCK, BLOCK), pl.ds(b * BLOCK, BLOCK)]
            else:
                tile = inner_part[pl.ds(b * BLOCK, BLOCK), pl.ds(a * BLOCK, BLOCK)].T
            part16[a, b] = rounded(tile)
    pick(0, OWN)
    term_sends[0].start()
    if not split:
        send_cross()

    def own_terms(i, carry):
        slot = 4 * OWN + i
        row = table[T_ITEM + slot]
        for p in range(WIDTH):
            terms[slot, p] = part16[row, table[T_POS + p]]
        return carry

    lax.fori_loop(0, OWN, own_terms, 0)
    kinetic_load.wait()

    def convert(s, carry):
        for k in range(NEIGH):
            coarse[s, :, pl.ds(k * BLOCK, BLOCK)] = kinetic[s, k].astype(BF16)
        return carry

    lax.fori_loop(0, OWN, convert, 0)
    for flow in sends:
        sends[flow].wait_send()
    for copy in second + third:
        copy.wait()
    for flow in term_receives:
        term_receives[flow].wait_recv()
    for flow in term_sends:
        term_sends[flow].wait_send()


def brick_stage(variant, count, table, orbitals, density_blocks, kinetic_blocks, hartree, vectors):
    caps, far, split, ident = variant
    any_spec = pl.BlockSpec(memory_space=pltpu.HBM)
    vmem_spec = pl.BlockSpec(memory_space=VMEM)
    pair = (WIDTH, BLOCK, BLOCK)
    points = orbitals.shape[2]
    dma = pltpu.SemaphoreType.DMA
    return pl.pallas_call(
        functools.partial(brick_kernel, caps, far, split, count),
        out_shape=(
            jax.ShapeDtypeStruct(hartree.shape, F32),
            jax.ShapeDtypeStruct((SLOTS,) + pair, BF16),
            jax.ShapeDtypeStruct((7 * OWN, BLOCK, VEC), BF16),
            jax.ShapeDtypeStruct(kinetic_blocks.shape, F32),
            jax.ShapeDtypeStruct((OWN, BLOCK, NEIGH * BLOCK), BF16),
        ),
        in_specs=[pl.BlockSpec(memory_space=SMEM)]
        + [any_spec, vmem_spec, any_spec, vmem_spec, vmem_spec],
        out_specs=(vmem_spec,) * 5,
        scratch_shapes=[
            VMEM((WIDTH, BLOCK, points), BF16),
            VMEM((4 * OWN,) + pair, BF16),
            VMEM((2 * OWN,) + pair, BF16),
            VMEM((3 * OWN,) + pair, BF16),
            VMEM((WIDTH * BLOCK, WIDTH * BLOCK), BF16),
            VMEM((PLANES, 1, PLANE), F32),
            VMEM((PLANES + 4, LINES, ROW), F32),
            VMEM((WIDTH, BLOCK, 2 * BLOCK), F32),
            VMEM((4 * BLOCK, 4 * BLOCK), F32),
            VMEM((WIDTH,) + pair, BF16),
            VMEM((4 * OWN,) + pair, BF16),
            dma((4,)),
            dma((4,)),
            dma((4,)),
            dma((2,)),
            dma((2,)),
            dma((4,)),
            dma((4,)),
            dma((6,)),
            dma((6,)),
        ],
        compiler_params=pltpu.CompilerParams(
            collective_id=ident, has_side_effects=True, vmem_limit_bytes=40 * 1024 * 1024
        ),
        name=f"bricks_{ident}",
    )(
        table,
        orbitals.reshape(WIDTH, BLOCK, points),
        density_blocks,
        kinetic_blocks,
        hartree,
        vectors,
    )


def sum_kernel(table, terms, kinetic, rounded, ham, coarse):
    del kinetic, rounded

    def add(slot, carry):
        @pl.when(table[T_VALID + slot] == 1)
        def _():
            s = table[T_ROW + slot]
            for p in range(WIDTH):
                k = table[T_PLACE + slot * WIDTH + p]
                total = ham[s, k] + terms[slot, p].astype(F32)
                ham[s, k] = total
                columns = pl.ds(pl.multiple_of(k * BLOCK, BLOCK), BLOCK)
                coarse[s, :, columns] = total.astype(BF16)

        return carry

    lax.fori_loop(0, SLOTS, add, 0)


def sum_stage(table, terms, kinetic, rounded):
    vmem_spec = pl.BlockSpec(memory_space=VMEM)
    return pl.pallas_call(
        sum_kernel,
        out_shape=(
            jax.ShapeDtypeStruct(kinetic.shape, F32),
            jax.ShapeDtypeStruct(rounded.shape, BF16),
        ),
        in_specs=[pl.BlockSpec(memory_space=SMEM)] + [vmem_spec] * 3,
        out_specs=(vmem_spec,) * 2,
        input_output_aliases={2: 0, 3: 1},
        compiler_params=pltpu.CompilerParams(vmem_limit_bytes=4 * 1024 * 1024),
        name="sum",
    )(table, terms, kinetic, rounded)


def row_product(table, s, coarse, held):
    rows = [held[table[T_LOOK + s * NEIGH + k]] for k in range(NEIGH)]
    return jnp.dot(coarse[s], jnp.concatenate(rows, axis=0), preferred_element_type=F32)


def first_kernel(far, count, table, coarse, vectors, held, send_sems, recv_sems):
    me = lax.axis_index("dev")
    step, partner, near, ahead, behind = around(me, count)
    friends = (partner, near, ahead, behind) if far else (partner, ahead, behind)
    greet(friends)
    first, second, third = vector_copies(held, send_sems, recv_sems, me, count, far)

    def row(s, carry):
        held[3 * OWN + s] = row_product(table, s, coarse, vectors).astype(BF16)
        return carry

    lax.fori_loop(0, OWN, row, 0)
    await_greetings(len(friends))
    for copy in first:
        copy.start()
    first[0].wait_recv()
    second[0].start()
    first[1].wait_recv()
    for copy in [second[1]] + third:
        copy.start()
    first[2].wait_recv()
    for copy in second + third:
        copy.wait_recv()
    for copy in first + second + third:
        copy.wait_send()


def first_stage(far, ident, count, table, coarse, vectors):
    vmem_spec = pl.BlockSpec(memory_space=VMEM)
    dma = pltpu.SemaphoreType.DMA
    return pl.pallas_call(
        functools.partial(first_kernel, far, count),
        out_shape=jax.ShapeDtypeStruct(vectors.shape, BF16),
        in_specs=[pl.BlockSpec(memory_space=SMEM)] + [vmem_spec] * 2,
        out_specs=vmem_spec,
        scratch_shapes=[dma((6,)), dma((6,))],
        compiler_params=pltpu.CompilerParams(
            collective_id=ident, has_side_effects=True, vmem_limit_bytes=8 * 1024 * 1024
        ),
        name=f"first_{ident}",
    )(table, coarse, vectors)


def second_kernel(
    table,
    held,
    coarse,
    vec_ref,
    ham,
    pot_ref,
    out_hbm,
    first_hbm,
    ham_hbm,
    pot_hbm,
    out,
    sems,
):
    copies = [
        pltpu.make_async_copy(pot_ref, pot_hbm, sems.at[OWN]),
        pltpu.make_async_copy(held.at[pl.ds(3 * OWN, OWN)], first_hbm, sems.at[OWN + 1]),
        pltpu.make_async_copy(ham, ham_hbm, sems.at[OWN + 2]),
    ]
    for copy in copies:
        copy.start()

    def store(s):
        return pltpu.make_async_copy(out.at[s], out_hbm.at[s], sems.at[s])

    def row(s, carry):
        total = row_product(table, s, coarse, held)
        out[s] = (2.0 * total - vec_ref[s].astype(F32)).astype(BF16)
        store(s).start()
        return carry

    lax.fori_loop(0, OWN, row, 0)
    for s in range(OWN):
        store(s).wait()
    for copy in copies:
        copy.wait()


def second_stage(table, held, coarse, vectors, ham, potential):
    vmem_spec = pl.BlockSpec(memory_space=VMEM)
    hbm_spec = pl.BlockSpec(memory_space=pltpu.HBM)
    blocks = jax.ShapeDtypeStruct((OWN, BLOCK, VEC), BF16)
    return pl.pallas_call(
        second_kernel,
        out_shape=(
            blocks,
            blocks,
            jax.ShapeDtypeStruct(ham.shape, F32),
            jax.ShapeDtypeStruct(potential.shape, F32),
        ),
        in_specs=[pl.BlockSpec(memory_space=SMEM)] + [vmem_spec] * 5,
        out_specs=(hbm_spec,) * 4,
        scratch_shapes=[
            VMEM(vectors.shape, BF16),
            pltpu.SemaphoreType.DMA((OWN + 3,)),
        ],
        compiler_params=pltpu.CompilerParams(vmem_limit_bytes=SECOND_LIMIT),
        name="second",
    )(table, held, coarse, vectors, ham, potential)


NARROW = ((OWN, 1, 1, 0), False, True, 1)
GENERAL = ((OWN, OWN, OWN, OWN), True, False, 2)
VARIANTS = (NARROW, GENERAL)


def per_device(
    orbitals, density_blocks, kinetic_blocks, hartree, vectors, brick_blocks, neighbours
):
    count = lax.axis_size("dev")
    table, level, density_rows, hartree_here, vector_blocks = prep_stage(
        count,
        brick_blocks,
        neighbours,
        density_blocks,
        hartree,
        vectors.reshape(OWN, BLOCK, VEC),
    )

    def program(variant):
        def branch():
            potential, terms, held, kinetic, rounded = brick_stage(
                variant,
                count,
                table,
                orbitals,
                density_rows,
                kinetic_blocks,
                hartree_here,
                vector_blocks,
            )
            ham, coarse = sum_stage(table, terms, kinetic, rounded)
            held_first = first_stage(variant[1], variant[3] + 2, count, table, coarse, held)
            second_term, first_term, hamiltonian, potential = second_stage(
                table, held_first, coarse, vector_blocks, ham, potential
            )
            return potential, hamiltonian, first_term, second_term

        return branch

    potential, hamiltonian, first_term, second_term = lax.switch(
        level[0], [program(v) for v in VARIANTS]
    )
    return (
        potential,
        hamiltonian,
        first_term.reshape(vectors.shape),
        second_term.reshape(vectors.shape),
    )


def solution(mesh):
    in_specs = (
        P("dev", None, None),
        P("dev", None, None, None),
        P("dev", None, None, None),
        P("dev", None, None),
        P("dev", None),
        P(),
        P(),
    )
    out_specs = (P("dev", None, None), P("dev", None, None, None), P("dev", None), P("dev", None))
    return jax.shard_map(
        per_device, mesh=mesh, in_specs=in_specs, out_specs=out_specs, check_vma=False
    )
```

profile of v0, /device:TPU:1, one launch (start us, length us, event | category | flops | bytes accessed | tf_op | source)
XLA Modules:
  0.0 62.9 jit_solution(2179992244151282140)
XLA Ops:
  0.6 3.6 %prep.1 = (s32[270]{0:T(512)S(1)}, s32[1]{0:T(128)}, bf16[4,16,128,128]{3,2,1,0:T(8,128)(2,1)S(1)}, f32[6,8,128]{2,1,0:T(8,128)S(1)}, bf16[4,128,256]{2,1,0:T(8,128)(2,1)S(1)}) custom-call(s32[6,128]{1,0:T(8,128)} %bitcast.13, s32[16,512]{1,0:T(8,128)} %bitcast.11, s32[6,128]{1,0:T(8,128)} %bitcast.14, s32[16,512]{1,0:T(8,128)} %bitcast.12, ...), custom_call_target="tpu_custom_call" | custom-call | tf_op jit(solution)/shard_map/prep/pallas_call | solution.py:238
  4.8 57.9 %conditional.1 = (f32[6,8,128]{2,1,0:T(8,128)}, f32[4,16,128,128]{3,2,1,0:T(8,128)}, bf16[4,128,256]{2,1,0:T(8,128)(2,1)}, bf16[4,128,256]{2,1,0:T(8,128)(2,1)}) conditional(s32[]{:T(128)} %bitcast.5, (bf16[1,768,6144]{2,1,0:T(8,128)(2,1)}, s32[270]{0:T(512)S(1)}, bf16[4,16,128,128]{3,2,1,0:T(8,128)(2,1)S(1)}, f32[4,16,128,128]{3,2,1,0:T(8,128)}, ...), branch_computations={%region_0.0_spmd, %region_1.0_spmd} | conditional | bytes 32 | solution.py:776
  4.9 37.3 %bricks_1.1 = (f32[6,8,128]{2,1,0:T(8,128)S(1)}, bf16[20,6,128,128]{3,2,1,0:T(8,128)(2,1)S(1)}, bf16[28,128,256]{2,1,0:T(8,128)(2,1)S(1)}, f32[4,16,128,128]{3,2,1,0:T(8,128)S(1)}, bf16[4,128,2048]{2,1,0:T(8,128)(2,1)S(1)}) custom-call(s32[270]{0:T(512)S(1)} %get-tuple-element.24.table, bf16[6,128,6144]{2,1,0:T(8,128)(2,1)} %bitcast.8, ...), custom_call_target="tpu_custom_call" | custom-call | tf_op jit(solution)/shard_map/cond/branch_0_fun/bricks_1/pallas_call | solution.py:545
  42.1 1.4 %sum.2 = (f32[4,16,128,128]{3,2,1,0:T(8,128)S(1)}, bf16[4,128,2048]{2,1,0:T(8,128)(2,1)S(1)}) custom-call(s32[270]{0:T(512)S(1)} %get-tuple-element.24.table, bf16[20,6,128,128]{3,2,1,0:T(8,128)(2,1)S(1)} %get-tuple-element.30.terms, f32[4,16,128,128]{3,2,1,0:T(8,128)S(1)} %get-tuple-element.31.kinetic, ...), custom_call_target="tpu_custom_call", output_to_operand_aliasing={{0}: (2, {}), {1}: (3, {})} | custom-call | tf_op jit(solution)/shard_map/cond/branch_0_fun/sum/pallas_call | solution.py:614
  43.5 16.2 %first_3.1.held = bf16[28,128,256]{2,1,0:T(8,128)(2,1)S(1)} custom-call(s32[270]{0:T(512)S(1)} %get-tuple-element.24.table, bf16[4,128,2048]{2,1,0:T(8,128)(2,1)S(1)} %get-tuple-element.33.coarse, bf16[28,128,256]{2,1,0:T(8,128)(2,1)S(1)} %get-tuple-element.34.vectors), custom_call_target="tpu_custom_call" | custom-call | tf_op jit(solution)/shard_map/cond/branch_0_fun/first_3/pallas_call | solution.py:663
  59.8 2.8 %second.2 = (bf16[4,128,256]{2,1,0:T(8,128)(2,1)}, bf16[4,128,256]{2,1,0:T(8,128)(2,1)}, f32[4,16,128,128]{3,2,1,0:T(8,128)}, f32[6,8,128]{2,1,0:T(8,128)}) custom-call(s32[270]{0:T(512)S(1)} %get-tuple-element.24.table, bf16[28,128,256]{2,1,0:T(8,128)(2,1)S(1)} %first_3.1.held, bf16[4,128,2048]{2,1,0:T(8,128)(2,1)S(1)} %get-tuple-element.33.coarse, ...), custom_call_target="tpu_custom_call" | custom-call | tf_op jit(solution)/shard_map/cond/branch_0_fun/second/pallas_call | solution.py:718
where the time goes:
time: 63.1 us; the launch traced here: 62.9 us
  Pallas kernels  61.2 us (97%)
  between operations  1.45 us (2%)
    pallas_call x1, Pallas kernels, brick_stage(): pl.pallas_call(functools.partial(brick_kernel, caps, far, split, count),...  37.3 us
    pallas_call x1, Pallas kernels, first_stage(): pl.pallas_call(functools.partial(first_kernel, far, count), out_shape=jax...  16.2 us
    pallas_call x1, Pallas kernels, prep_stage(): pl.pallas_call(functools.partial(prep_kernel, count), out_shape=(jax.Shap...  3.55 us
    pallas_call x1, Pallas kernels, second_stage(): pl.pallas_call(second_kernel, out_shape=(blocks, blocks, jax.ShapeDtypeSt...  2.79 us
    pallas_call x1, Pallas kernels, sum_stage(): pl.pallas_call(sum_kernel, out_shape=(jax.ShapeDtypeStruct(kinetic.shape,...  1.36 us

commit v1 on v0

--- a/solution.py
+++ b/solution.py
@@ -22,6 +22,7 @@
 
 BLOCK = 128
 OWN = 4
+BITS = 2
 WIDTH = 6
 NEIGH = 16
 PLANES = 6
@@ -34,6 +35,8 @@
 PREP_LIMIT = 60_900_000
 
 FLOWS = 5
+HALF = OWN // 2
+FLIGHTS = 6
 SLOTS = FLOWS * OWN
 BACK = (0, 1, 3, 2)
 
@@ -45,7 +48,11 @@
 T_POS = T_PERM + WIDTH
 T_ITEM = T_POS + WIDTH
 T_LOOK = T_ITEM + SLOTS
-T_SIZE = T_LOOK + OWN * NEIGH
+T_GET = T_LOOK + OWN * NEIGH
+T_SPARE = T_GET + FLOWS * OWN * NEIGH
+T_SIZE = T_SPARE + 1
+CLOSE = 2 * OWN * WIDTH
+CROSS = 3 * OWN * WIDTH
 SPAN = 9 * OWN
 
 
@@ -80,34 +87,33 @@
     )
 
 
-def row_copies(send, place, send_sems, recv_sems, caps, devices):
+def row_copies(source, place, send_sems, recv_sems, caps, devices):
     sends, receives = {}, {}
     for flow in range(4):
         back = BACK[flow]
         if caps[flow]:
-            slots = pl.ds(flow * OWN, caps[flow])
-            there = place(back, caps[flow])
+            here, there = source(flow, caps[flow]), place(back, caps[flow])
             sends[flow] = remote(
-                send.at[slots], there, send_sems.at[flow], recv_sems.at[back], devices[flow]
+                here, there, send_sems.at[flow], recv_sems.at[back], devices[flow]
             )
         if caps[back]:
-            slots = pl.ds(flow * OWN, caps[back])
-            here = place(flow, caps[back])
+            gone, here = source(flow, caps[back]), place(flow, caps[back])
             receives[flow] = remote(
-                send.at[slots], here, send_sems.at[flow], recv_sems.at[flow], devices[flow]
+                gone, here, send_sems.at[flow], recv_sems.at[flow], devices[flow]
             )
     return sends, receives
 
 
-def vector_copies(held, send_sems, recv_sems, me, count, far):
+def vector_copies(held, send_sems, recv_sems, me, count, far, part):
     step, partner, near, ahead, behind = around(me, count)
     up = lax.rem(me + 2, count)
     down = lax.rem(me + count - 2, count)
 
     def piece(delta):
-        return held.at[pl.ds((delta + 3) * OWN, OWN)]
+        return held.at[pl.ds((delta + 3) * OWN + part * HALF, HALF)]
 
     def copy(src_delta, dst_delta, sem, device):
+        sem = part * FLIGHTS + sem
         return remote(
             piece(src_delta), piece(dst_delta), send_sems.at[sem], recv_sems.at[sem], device
         )
@@ -147,7 +153,8 @@
     loads = [
         pltpu.make_async_copy(src, dst, sems.at[i])
         for i, (src, dst) in enumerate(
-            ((blocks_hbm, blocks), (hartree_hbm, hartree), (vec_hbm, vec))
+            [(blocks_hbm.at[s], blocks.at[s]) for s in range(OWN)]
+            + [(hartree_hbm, hartree), (vec_hbm, vec)]
         )
     ]
     for load in loads:
@@ -160,19 +167,20 @@
     width = brick_rows.shape
     lists = brick_rows[...]
     brick = lax.broadcasted_iota(jnp.int32, width, 1)
-    owner = lists // OWN
+    owner = lists >> BITS
     rank = jnp.ones(width, jnp.int32)
     for j in range(WIDTH):
         one = jnp.broadcast_to(lists[j : j + 1], width)
-        rank += jnp.where((one // OWN == owner) & (one < lists), 1, 0)
+        rank += jnp.where((one >> BITS == owner) & (one < lists), 1, 0)
     delta = owner - brick
     delta = jnp.where(delta > count // 2, delta - count, delta)
     delta = jnp.where(delta < -(count // 2), delta + count, delta)
-    sided = jnp.where(brick % 2 == 0, delta, -delta)
-    near_rows = jnp.max(jnp.where(sided < 0, rank, 0))
+    sided = jnp.where((brick & 1) == 0, delta, -delta)
+    from_near = jnp.sum(jnp.where(sided < 0, 1, 0), axis=0, keepdims=True)
+    near_rows = jnp.max(from_near)
     far_rows = jnp.max(jnp.where(sided > 1, rank, 0))
-    used = neigh_rows[...] // (2 * OWN)
-    home = lax.broadcasted_iota(jnp.int32, used.shape, 1) // (2 * OWN)
+    used = neigh_rows[...] >> (BITS + 1)
+    home = lax.broadcasted_iota(jnp.int32, used.shape, 1) >> (BITS + 1)
     apart = jnp.abs(used - home)
     apart = jnp.minimum(apart, count // 2 - apart)
     chips = jnp.max(apart)
@@ -184,8 +192,11 @@
         gap = jnp.where(gap < 0, gap + blocks, gap)
         return jnp.where(gap >= blocks, gap - blocks, gap)
 
-    for q in range(T_SIZE):
+    for q in (*range(T_SLOT), *range(T_ITEM, T_LOOK)):
         table[q] = 0
+    for f in range(FLOWS):
+        for q in range(OWN * NEIGH):
+            table[T_GET + f * OWN * NEIGH + q] = CLOSE if f in (0, 4) else CROSS
     for s in range(OWN):
         for k in range(NEIGH):
             gap = near_id(neigh[k, me * OWN + s])
@@ -203,13 +214,16 @@
             table[T_ROW + slot] = s
             table[T_VALID + slot] = 1
             for p in range(WIDTH):
-                gap = jnp.where(hit, s * SPAN + gaps[p], 0)
-                table[T_PLACE + slot * WIDTH + p] = inverse[gap]
+                k = inverse[jnp.where(hit, s * SPAN + gaps[p], 0)]
+                table[T_PLACE + slot * WIDTH + p] = k
+                first_slot = {0: 0, 4: OWN}.get(f, (f - 1) * OWN)
+                spot = T_GET + (f * OWN + s) * NEIGH + k
+                table[jnp.where(hit, spot, T_SPARE)] = (first_slot + found) * WIDTH + p
             found = found + jnp.where(hit, 1, 0)
 
     listed = [bricks[p, me] for p in range(WIDTH)]
-    owners = [b // OWN for b in listed]
-    local = [jnp.where(o // 2 == me // 2, 1, 0) for o in owners]
+    owners = [b >> BITS for b in listed]
+    local = [jnp.where(o >> 1 == me >> 1, 1, 0) for o in owners]
     ahead = 0
     behind = sum(local)
     for j in range(WIDTH):
@@ -246,10 +260,15 @@
         ),
         in_specs=[smem_spec, smem_spec, vmem_spec, vmem_spec] + [hbm_spec] * 3,
         out_specs=(smem_spec, smem_spec) + (vmem_spec,) * 3,
-        scratch_shapes=[SMEM((OWN * SPAN,), jnp.int32), pltpu.SemaphoreType.DMA((3,))],
+        scratch_shapes=[SMEM((OWN * SPAN,), jnp.int32), pltpu.SemaphoreType.DMA((OWN + 2,))],
         compiler_params=pltpu.CompilerParams(vmem_limit_bytes=PREP_LIMIT),
         name="prep",
     )(brick_blocks, neighbours, brick_blocks, neighbours, density_blocks, hartree, vectors)
+
+
+def row_product(table, s, coarse, held):
+    rows = [held[table[T_LOOK + s * NEIGH + k]] for k in range(NEIGH)]
+    return jnp.dot(coarse[s], jnp.concatenate(rows, axis=0), preferred_element_type=F32)
 
 
 def brick_kernel(
@@ -264,10 +283,14 @@
     hartree_ref,
     vec_ref,
     pot_ref,
-    terms,
+    held_first,
+    ham,
+    coarse,
     held,
-    kinetic,
-    coarse,
+    close_terms,
+    cross_terms,
+    first_send_sems,
+    first_recv_sems,
     orb,
     send,
     close,
@@ -279,7 +302,10 @@
     inner_part,
     part16,
     tsend,
+    other,
     local_sems,
+    side_send_sems,
+    side_recv_sems,
     send_sems,
     recv_sems,
     halo_send_sems,
@@ -313,23 +339,38 @@
             return close.at[pl.ds(0, slots)]
         return cross.at[pl.ds((flow - 1) * OWN, slots)]
 
-    sends, receives = row_copies(send, row_place, send_sems, recv_sems, caps, devices)
+    def row_source(flow, slots):
+        return send.at[pl.ds(flow * OWN, slots)]
+
+    sends, receives = row_copies(row_source, row_place, send_sems, recv_sems, caps, devices)
     for flow in (1, 2, 3):
         fill(send, flow * OWN, flow, caps[flow])
+    if split:
+        fill(send, 2 * OWN, 2, 1)
+    fill(send, 0, 0, OWN)
+    fill(close, OWN, 4, OWN)
     await_greetings(4)
-    for flow in (1, 2, 3):
-        if flow in sends:
+    swap = remote(
+        send.at[pl.ds(2 * OWN, 1)], other, side_send_sems.at[0], side_recv_sems.at[0], partner
+    )
+    if split:
+        swap.start()
+        sends[0].start()
+        swap.wait()
+        mine = table[T_VALID + OWN] == 1
+        for p in range(WIDTH):
+            send[OWN, p] = jnp.where(mine, send[OWN, p], other[0, p])
+        sends[1].start()
+    else:
+        for flow in (1, 2, 3, 0):
             sends[flow].start()
-    fill(send, 0, 0, OWN)
-    sends[0].start()
-    fill(close, OWN, 4, OWN)
-    kinetic_load = pltpu.make_async_copy(kinetic_hbm, kinetic, local_sems.at[3])
+    kinetic_load = pltpu.make_async_copy(kinetic_hbm, ham, local_sems.at[3])
     kinetic_load.start()
 
     def assemble(rows, all_here):
         for a in rows:
             slot = table[T_SLOT + a]
-            far_slot = jnp.clip(slot - OWN, 0, 3 * OWN - 1)
+            far_slot = 0 if split else jnp.clip(slot - OWN, 0, 3 * OWN - 1)
             is_far = (slot >= OWN) & (slot < 4 * OWN)
             close_slot = jnp.where(slot < OWN, slot, jnp.maximum(slot - 3 * OWN, 0))
             for p in range(WIDTH):
@@ -344,7 +385,14 @@
                 receives[flow].wait_recv()
 
     own_vec.wait()
-    first, second, third = vector_copies(held, vec_send_sems, vec_recv_sems, me, count, far)
+    parts = [
+        vector_copies(held, vec_send_sems, vec_recv_sems, me, count, far, part)
+        for part in range(2)
+    ]
+
+    def start_vectors(part):
+        for copy in parts[part][0]:
+            copy.start()
 
     def row_terms(x, begin, end):
         cols = pl.ds(pl.multiple_of(x * PLANE, PLANE), PLANE)
@@ -385,6 +433,7 @@
     if split:
         await_cross()
     assemble(range(4, WIDTH), True)
+    start_vectors(0)
     lax.fori_loop(0, 4, outer_body, 0)
     below = lax.rem(me + count - 1, count)
     above = lax.rem(me + 1, count)
@@ -396,8 +445,7 @@
     )
     halo_down.start()
     halo_up.start()
-    for copy in first:
-        copy.start()
+    start_vectors(1)
     lax.fori_loop(5, 6, inner_body, 0)
     lax.fori_loop(4, 6, outer_body, 0)
     outer_part[...] = jnp.zeros_like(outer_part)
@@ -466,36 +514,36 @@
             if b < 4:
                 part16[b, a] = rounded(tile)
 
-    def pick(flow, slots):
+    def pick(flow, slots, target, base):
         def body(i, carry):
-            slot = flow * OWN + i
-            row = table[T_ITEM + slot]
+            row = WIDTH - 1 if split and flow in (1, 2, 3) else table[T_ITEM + flow * OWN + i]
             for p in range(WIDTH):
-                tsend[slot, p] = part16[row, table[T_POS + p]]
+                target[base + i * WIDTH + p] = part16[row, table[T_POS + p]]
             return carry
 
         lax.fori_loop(0, slots, body, 0)
 
+    def term_source(flow, slots):
+        return tsend.at[pl.ds(flow * OWN * WIDTH, slots * WIDTH)]
+
     def term_place(flow, slots):
-        return terms.at[pl.ds(flow * OWN, slots)]
+        if flow == 0:
+            return close_terms.at[pl.ds(0, slots * WIDTH)]
+        return cross_terms.at[pl.ds((flow - 1) * OWN * WIDTH, slots * WIDTH)]
 
     term_caps = [caps[BACK[flow]] for flow in range(4)]
     term_sends, term_receives = row_copies(
-        tsend, term_place, term_send_sems, term_recv_sems, term_caps, devices
+        term_source, term_place, term_send_sems, term_recv_sems, term_caps, devices
     )
 
     def send_cross():
         for flow in (1, 3, 2):
             if flow in term_sends:
-                pick(flow, term_caps[flow])
+                pick(flow, term_caps[flow], tsend, flow * OWN * WIDTH)
                 term_sends[flow].start()
 
     if split:
         send_cross()
-    for copy in first:
-        copy.wait()
-    for copy in second + third:
-        copy.start()
     lax.fori_loop(0, PLANES // STEP, inner_terms, 0)
     for a in range(4):
         for b in range(4):
@@ -504,33 +552,80 @@
             else:
                 tile = inner_part[pl.ds(b * BLOCK, BLOCK), pl.ds(a * BLOCK, BLOCK)].T
             part16[a, b] = rounded(tile)
-    pick(0, OWN)
+    pick(0, OWN, tsend, 0)
     term_sends[0].start()
     if not split:
         send_cross()
-
-    def own_terms(i, carry):
-        slot = 4 * OWN + i
-        row = table[T_ITEM + slot]
-        for p in range(WIDTH):
-            terms[slot, p] = part16[row, table[T_POS + p]]
+    for first, second, third in parts:
+        for copy in first:
+            copy.wait()
+        for copy in second + third:
+            copy.start()
+
+    pick(4, OWN, close_terms, OWN * WIDTH)
+    close_terms[CLOSE] = jnp.zeros((BLOCK, BLOCK), BF16)
+    cross_terms[CROSS] = jnp.zeros((BLOCK, BLOCK), BF16)
+
+    def term(source, flow, s, k):
+        return source[table[T_GET + (flow * OWN + s) * NEIGH + k]].astype(F32)
+
+    def close_row(s, carry):
+        for k in range(NEIGH):
+            ham[s, k] = ham[s, k] + term(close_terms, 4, s, k) + term(close_terms, 0, s, k)
         return carry
 
-    lax.fori_loop(0, OWN, own_terms, 0)
+    def last_row(s, carry):
+        for k in range(NEIGH):
+            total = ham[s, k]
+            for flow in (1, 2) if split else (1, 2, 3):
+                total = total + term(cross_terms, flow, s, k)
+            ham[s, k] = total
+            coarse[s, :, pl.ds(k * BLOCK, BLOCK)] = total.astype(BF16)
+        held_first[3 * OWN + s] = row_product(table, s, coarse, held).astype(BF16)
+        return carry
+
+    forward = remote(
+        cross_terms.at[pl.ds(0, WIDTH)],
+        cross_terms.at[pl.ds(OWN * WIDTH, WIDTH)],
+        side_send_sems.at[1],
+        side_recv_sems.at[1],
+        partner,
+    )
     kinetic_load.wait()
-
-    def convert(s, carry):
-        for k in range(NEIGH):
-            coarse[s, :, pl.ds(k * BLOCK, BLOCK)] = kinetic[s, k].astype(BF16)
-        return carry
-
-    lax.fori_loop(0, OWN, convert, 0)
+    term_receives[0].wait_recv()
+    lax.fori_loop(0, OWN, close_row, 0)
+    if split:
+        term_receives[1].wait_recv()
+        forward.start()
+        forward.wait()
+    else:
+        for flow in (1, 2, 3):
+            term_receives[flow].wait_recv()
+    for first, second, third in parts:
+        for copy in second + third:
+            copy.wait()
+
+    parts = [
+        vector_copies(held_first, first_send_sems, first_recv_sems, me, count, far, part)
+        for part in range(2)
+    ]
+    for part in range(2):
+        lax.fori_loop(part * HALF, (part + 1) * HALF, last_row, 0)
+        start_vectors(part)
+    for first, second, third in parts:
+        first[0].wait_recv()
+        second[0].start()
+        first[1].wait_recv()
+        for copy in [second[1]] + third:
+            copy.start()
+    for first, second, third in parts:
+        first[2].wait_recv()
+        for copy in second + third:
+            copy.wait_recv()
+        for copy in first + second + third:
+            copy.wait_send()
     for flow in sends:
         sends[flow].wait_send()
-    for copy in second + third:
-        copy.wait()
-    for flow in term_receives:
-        term_receives[flow].wait_recv()
     for flow in term_sends:
         term_sends[flow].wait_send()
 
@@ -546,15 +641,19 @@
         functools.partial(brick_kernel, caps, far, split, count),
         out_shape=(
             jax.ShapeDtypeStruct(hartree.shape, F32),
-            jax.ShapeDtypeStruct((SLOTS,) + pair, BF16),
             jax.ShapeDtypeStruct((7 * OWN, BLOCK, VEC), BF16),
             jax.ShapeDtypeStruct(kinetic_blocks.shape, F32),
             jax.ShapeDtypeStruct((OWN, BLOCK, NEIGH * BLOCK), BF16),
         ),
         in_specs=[pl.BlockSpec(memory_space=SMEM)]
         + [any_spec, vmem_spec, any_spec, vmem_spec, vmem_spec],
-        out_specs=(vmem_spec,) * 5,
+        out_specs=(vmem_spec,) * 4,
         scratch_shapes=[
+            VMEM((7 * OWN, BLOCK, VEC), BF16),
+            VMEM((CLOSE + 1, BLOCK, BLOCK), BF16),
+            VMEM((CROSS + 1, BLOCK, BLOCK), BF16),
+            dma((2 * FLIGHTS,)),
+            dma((2 * FLIGHTS,)),
             VMEM((WIDTH, BLOCK, points), BF16),
             VMEM((4 * OWN,) + pair, BF16),
             VMEM((2 * OWN,) + pair, BF16),
@@ -565,16 +664,19 @@
             VMEM((WIDTH, BLOCK, 2 * BLOCK), F32),
             VMEM((4 * BLOCK, 4 * BLOCK), F32),
             VMEM((WIDTH,) + pair, BF16),
-            VMEM((4 * OWN,) + pair, BF16),
+            VMEM((4 * OWN * WIDTH, BLOCK, BLOCK), BF16),
+            VMEM((1,) + pair, BF16),
             dma((4,)),
+            dma((2,)),
+            dma((2,)),
             dma((4,)),
             dma((4,)),
             dma((2,)),
             dma((2,)),
             dma((4,)),
             dma((4,)),
-            dma((6,)),
-            dma((6,)),
+            dma((2 * FLIGHTS,)),
+            dma((2 * FLIGHTS,)),
         ],
         compiler_params=pltpu.CompilerParams(
             collective_id=ident, has_side_effects=True, vmem_limit_bytes=40 * 1024 * 1024
@@ -588,89 +690,6 @@
         hartree,
         vectors,
     )
-
-
-def sum_kernel(table, terms, kinetic, rounded, ham, coarse):
-    del kinetic, rounded
-
-    def add(slot, carry):
-        @pl.when(table[T_VALID + slot] == 1)
-        def _():
-            s = table[T_ROW + slot]
-            for p in range(WIDTH):
-                k = table[T_PLACE + slot * WIDTH + p]
-                total = ham[s, k] + terms[slot, p].astype(F32)
-                ham[s, k] = total
-                columns = pl.ds(pl.multiple_of(k * BLOCK, BLOCK), BLOCK)
-                coarse[s, :, columns] = total.astype(BF16)
-
-        return carry
-
-    lax.fori_loop(0, SLOTS, add, 0)
-
-
-def sum_stage(table, terms, kinetic, rounded):
-    vmem_spec = pl.BlockSpec(memory_space=VMEM)
-    return pl.pallas_call(
-        sum_kernel,
-        out_shape=(
-            jax.ShapeDtypeStruct(kinetic.shape, F32),
-            jax.ShapeDtypeStruct(rounded.shape, BF16),
-        ),
-        in_specs=[pl.BlockSpec(memory_space=SMEM)] + [vmem_spec] * 3,
-        out_specs=(vmem_spec,) * 2,
-        input_output_aliases={2: 0, 3: 1},
-        compiler_params=pltpu.CompilerParams(vmem_limit_bytes=4 * 1024 * 1024),
-        name="sum",
-    )(table, terms, kinetic, rounded)
-
-
-def row_product(table, s, coarse, held):
-    rows = [held[table[T_LOOK + s * NEIGH + k]] for k in range(NEIGH)]
-    return jnp.dot(coarse[s], jnp.concatenate(rows, axis=0), preferred_element_type=F32)
-
-
-def first_kernel(far, count, table, coarse, vectors, held, send_sems, recv_sems):
-    me = lax.axis_index("dev")
-    step, partner, near, ahead, behind = around(me, count)
-    friends = (partner, near, ahead, behind) if far else (partner, ahead, behind)
-    greet(friends)
-    first, second, third = vector_copies(held, send_sems, recv_sems, me, count, far)
-
-    def row(s, carry):
-        held[3 * OWN + s] = row_product(table, s, coarse, vectors).astype(BF16)
-        return carry
-
-    lax.fori_loop(0, OWN, row, 0)
-    await_greetings(len(friends))
-    for copy in first:
-        copy.start()
-    first[0].wait_recv()
-    second[0].start()
-    first[1].wait_recv()
-    for copy in [second[1]] + third:
-        copy.start()
-    first[2].wait_recv()
-    for copy in second + third:
-        copy.wait_recv()
-    for copy in first + second + third:
-        copy.wait_send()
-
-
-def first_stage(far, ident, count, table, coarse, vectors):
-    vmem_spec = pl.BlockSpec(memory_space=VMEM)
-    dma = pltpu.SemaphoreType.DMA
-    return pl.pallas_call(
-        functools.partial(first_kernel, far, count),
-        out_shape=jax.ShapeDtypeStruct(vectors.shape, BF16),
-        in_specs=[pl.BlockSpec(memory_space=SMEM)] + [vmem_spec] * 2,
-        out_specs=vmem_spec,
-        scratch_shapes=[dma((6,)), dma((6,))],
-        compiler_params=pltpu.CompilerParams(
-            collective_id=ident, has_side_effects=True, vmem_limit_bytes=8 * 1024 * 1024
-        ),
-        name=f"first_{ident}",
-    )(table, coarse, vectors)
 
 
 def second_kernel(
@@ -734,7 +753,7 @@
     )(table, held, coarse, vectors, ham, potential)
 
 
-NARROW = ((OWN, 1, 1, 0), False, True, 1)
+NARROW = ((OWN, 1, 0, 0), False, True, 1)
 GENERAL = ((OWN, OWN, OWN, OWN), True, False, 2)
 VARIANTS = (NARROW, GENERAL)
 
@@ -754,7 +773,7 @@
 
     def program(variant):
         def branch():
-            potential, terms, held, kinetic, rounded = brick_stage(
+            potential, held_first, ham, coarse = brick_stage(
                 variant,
                 count,
                 table,
@@ -764,8 +783,6 @@
                 hartree_here,
                 vector_blocks,
             )
-            ham, coarse = sum_stage(table, terms, kinetic, rounded)
-            held_first = first_stage(variant[1], variant[3] + 2, count, table, coarse, held)
             second_term, first_term, hamiltonian, potential = second_stage(
                 table, held_first, coarse, vector_blocks, ham, potential
             )

time: 63.1 us -> 59.7 us (0.946)
  Pallas kernels: 61.2 us -> 57.8 us
    pallas_call x2 -> x0, Pallas kernels: 17.6 us -> none  [the longest x1 16.2 us: first_stage(): pl.pallas_call(functools.partial(first_kernel, far, count), out_shape=jax...]
    pallas_call x1, Pallas kernels: 37.3 us -> 51.3 us  [brick_stage(): pl.pallas_call(functools.partial(brick_kernel, caps, far, split, count),...]
where the time goes in v1:
time: 59.7 us; the launch traced here: 59.5 us
  Pallas kernels  57.8 us (97%)
  between operations  1.45 us (2%)
    pallas_call x1, Pallas kernels, brick_stage(): pl.pallas_call(functools.partial(brick_kernel, caps, far, split, count),...  51.3 us
    pallas_call x1, Pallas kernels, prep_stage(): pl.pallas_call(functools.partial(prep_kernel, count), out_shape=(jax.Shap...  3.68 us
    pallas_call x1, Pallas kernels, second_stage(): pl.pallas_call(second_kernel, out_shape=(blocks, blocks, jax.ShapeDtypeSt...  2.8 us

profile of v1, /device:TPU:1, one launch (start us, length us, event | category | flops | bytes accessed | tf_op | source)
XLA Modules:
  0.0 59.5 jit_solution(6003343577872158825)
XLA Ops:
  0.6 3.7 %prep.1 = (s32[591]{0:T(1024)S(1)}, s32[1]{0:T(128)}, bf16[4,16,128,128]{3,2,1,0:T(8,128)(2,1)S(1)}, f32[6,8,128]{2,1,0:T(8,128)S(1)}, bf16[4,128,256]{2,1,0:T(8,128)(2,1)S(1)}) custom-call(s32[6,128]{1,0:T(8,128)} %bitcast.13, s32[16,512]{1,0:T(8,128)} %bitcast.11, s32[6,128]{1,0:T(8,128)} %bitcast.14, s32[16,512]{1,0:T(8,128)} %bitcast.12, ...), custom_call_target="tpu_custom_call" | custom-call | tf_op jit(solution)/shard_map/prep/pallas_call | solution.py:252
  5.0 54.3 %conditional.1 = (f32[6,8,128]{2,1,0:T(8,128)}, f32[4,16,128,128]{3,2,1,0:T(8,128)}, bf16[4,128,256]{2,1,0:T(8,128)(2,1)}, bf16[4,128,256]{2,1,0:T(8,128)(2,1)}) conditional(s32[]{:T(128)} %bitcast.5, (bf16[1,768,6144]{2,1,0:T(8,128)(2,1)}, s32[591]{0:T(1024)S(1)}, bf16[4,16,128,128]{3,2,1,0:T(8,128)(2,1)S(1)}, f32[4,16,128,128]{3,2,1,0:T(8,128)}, ...), branch_computations={%region_0.0_spmd, %region_1.0_spmd} | conditional | bytes 32 | solution.py:793
  5.0 51.3 %bricks_1.1 = (f32[6,8,128]{2,1,0:T(8,128)S(1)}, bf16[28,128,256]{2,1,0:T(8,128)(2,1)S(1)}, f32[4,16,128,128]{3,2,1,0:T(8,128)S(1)}, bf16[4,128,2048]{2,1,0:T(8,128)(2,1)S(1)}) custom-call(s32[591]{0:T(1024)S(1)} %get-tuple-element.24.table, bf16[6,128,6144]{2,1,0:T(8,128)(2,1)} %bitcast.8, bf16[4,16,128,128]{3,2,1,0:T(8,128)(2,1)S(1)} %get-tuple-element.26.blocks, ...), custom_call_target="tpu_custom_call" | custom-call | tf_op jit(solution)/shard_map/cond/branch_0_fun/bricks_1/pallas_call | solution.py:640
  56.3 2.8 %second.2 = (bf16[4,128,256]{2,1,0:T(8,128)(2,1)}, bf16[4,128,256]{2,1,0:T(8,128)(2,1)}, f32[4,16,128,128]{3,2,1,0:T(8,128)}, f32[6,8,128]{2,1,0:T(8,128)}) custom-call(s32[591]{0:T(1024)S(1)} %get-tuple-element.24.table, bf16[28,128,256]{2,1,0:T(8,128)(2,1)S(1)} %get-tuple-element.30.held, bf16[4,128,2048]{2,1,0:T(8,128)(2,1)S(1)} %get-tuple-element.31.coarse, ...), custom_call_target="tpu_custom_call" | custom-call | tf_op jit(solution)/shard_map/cond/branch_0_fun/second/pallas_call | solution.py:737

commit v2 on v1

--- a/solution.py
+++ b/solution.py
@@ -433,7 +433,6 @@
     if split:
         await_cross()
     assemble(range(4, WIDTH), True)
-    start_vectors(0)
     lax.fori_loop(0, 4, outer_body, 0)
     below = lax.rem(me + count - 1, count)
     above = lax.rem(me + 1, count)
@@ -445,6 +444,7 @@
     )
     halo_down.start()
     halo_up.start()
+    start_vectors(0)
     start_vectors(1)
     lax.fori_loop(5, 6, inner_body, 0)
     lax.fori_loop(4, 6, outer_body, 0)

time: 59.7 us -> 59.6 us (level)
  no operation moved by 1% of the time
where the time goes in v2:
time: 59.6 us; the launch traced here: 59.3 us
  Pallas kernels  57.7 us (97%)
  between operations  1.45 us (2%)
    pallas_call x1, Pallas kernels, brick_stage(): pl.pallas_call(functools.partial(brick_kernel, caps, far, split, count),...  51.2 us
    pallas_call x1, Pallas kernels, prep_stage(): pl.pallas_call(functools.partial(prep_kernel, count), out_shape=(jax.Shap...  3.68 us
    pallas_call x1, Pallas kernels, second_stage(): pl.pallas_call(second_kernel, out_shape=(blocks, blocks, jax.ShapeDtypeSt...  2.8 us

profile of v2, /device:TPU:1, one launch (start us, length us, event | category | flops | bytes accessed | tf_op | source)
XLA Modules:
  0.0 59.3 jit_solution(17507730658955039656)
XLA Ops:
  0.6 3.7 %prep.1 = (s32[591]{0:T(1024)S(1)}, s32[1]{0:T(128)}, bf16[4,16,128,128]{3,2,1,0:T(8,128)(2,1)S(1)}, f32[6,8,128]{2,1,0:T(8,128)S(1)}, bf16[4,128,256]{2,1,0:T(8,128)(2,1)S(1)}) custom-call(s32[6,128]{1,0:T(8,128)} %bitcast.13, s32[16,512]{1,0:T(8,128)} %bitcast.11, s32[6,128]{1,0:T(8,128)} %bitcast.14, s32[16,512]{1,0:T(8,128)} %bitcast.12, ...), custom_call_target="tpu_custom_call" | custom-call | tf_op jit(solution)/shard_map/prep/pallas_call | solution.py:252
  5.0 54.2 %conditional.1 = (f32[6,8,128]{2,1,0:T(8,128)}, f32[4,16,128,128]{3,2,1,0:T(8,128)}, bf16[4,128,256]{2,1,0:T(8,128)(2,1)}, bf16[4,128,256]{2,1,0:T(8,128)(2,1)}) conditional(s32[]{:T(128)} %bitcast.5, (bf16[1,768,6144]{2,1,0:T(8,128)(2,1)}, s32[591]{0:T(1024)S(1)}, bf16[4,16,128,128]{3,2,1,0:T(8,128)(2,1)S(1)}, f32[4,16,128,128]{3,2,1,0:T(8,128)}, ...), branch_computations={%region_0.0_spmd, %region_1.0_spmd} | conditional | bytes 32 | solution.py:793
  5.0 51.2 %bricks_1.1 = (f32[6,8,128]{2,1,0:T(8,128)S(1)}, bf16[28,128,256]{2,1,0:T(8,128)(2,1)S(1)}, f32[4,16,128,128]{3,2,1,0:T(8,128)S(1)}, bf16[4,128,2048]{2,1,0:T(8,128)(2,1)S(1)}) custom-call(s32[591]{0:T(1024)S(1)} %get-tuple-element.24.table, bf16[6,128,6144]{2,1,0:T(8,128)(2,1)} %bitcast.8, bf16[4,16,128,128]{3,2,1,0:T(8,128)(2,1)S(1)} %get-tuple-element.26.blocks, ...), custom_call_target="tpu_custom_call" | custom-call | tf_op jit(solution)/shard_map/cond/branch_0_fun/bricks_1/pallas_call | solution.py:640
  56.2 2.8 %second.2 = (bf16[4,128,256]{2,1,0:T(8,128)(2,1)}, bf16[4,128,256]{2,1,0:T(8,128)(2,1)}, f32[4,16,128,128]{3,2,1,0:T(8,128)}, f32[6,8,128]{2,1,0:T(8,128)}) custom-call(s32[591]{0:T(1024)S(1)} %get-tuple-element.24.table, bf16[28,128,256]{2,1,0:T(8,128)(2,1)S(1)} %get-tuple-element.30.held, bf16[4,128,2048]{2,1,0:T(8,128)(2,1)S(1)} %get-tuple-element.31.coarse, ...), custom_call_target="tpu_custom_call" | custom-call | tf_op jit(solution)/shard_map/cond/branch_0_fun/second/pallas_call | solution.py:737
